TPU v7x, 16 devices: a 4x2x1 block of a 4x4x8 slice. The times are simulated.
16 devices in a mesh: rep: 4 (over y, z, core), dp: 4 (over x).
Axes of the slice: x: 4, y: 2, z: 1, core: 2. Of those that a mesh axis runs over, the one named last changes fastest.
The devices are a block of a 4x4x8 slice.
Arguments:
- x: bfloat16 [16, 2048, 1280], P(('rep', 'dp')), parts along dimension 0
- dy: bfloat16 [16, 2048, 1280], P(('rep', 'dp')), parts along dimension 0
- w_gate: bfloat16 [2, 1280, 3456], P(None, 'dp')
- w_up: bfloat16 [2, 1280, 3456], P(None, 'dp')
- w_down: bfloat16 [2, 3456, 1280], P(None, 'dp')
- m_w_gate: float32 [2, 1280, 3456], P(None, 'dp')
- m_w_up: float32 [2, 1280, 3456], P(None, 'dp')
- m_w_down: float32 [2, 3456, 1280], P(None, 'dp')
- v_w_gate: float32 [2, 1280, 3456], P(None, 'dp')
- v_w_up: float32 [2, 1280, 3456], P(None, 'dp')
- v_w_down: float32 [2, 3456, 1280], P(None, 'dp')
Outputs:
- output 1: bfloat16 [8, 1280, 3456], P('rep', 'dp'), parts along dimension 0
- output 2: bfloat16 [8, 1280, 3456], P('rep', 'dp'), parts along dimension 0
- output 3: bfloat16 [8, 3456, 1280], P('rep', 'dp'), parts along dimension 0
- output 4: float32 [8, 1280, 3456], P('rep', 'dp'), parts along dimension 0
- output 5: float32 [8, 1280, 3456], P('rep', 'dp'), parts along dimension 0
- output 6: float32 [8, 3456, 1280], P('rep', 'dp'), parts along dimension 0
- output 7: float32 [8, 1280, 3456], P('rep', 'dp'), parts along dimension 0
- output 8: float32 [8, 1280, 3456], P('rep', 'dp'), parts along dimension 0
- output 9: float32 [8, 3456, 1280], P('rep', 'dp'), parts along dimension 0
There are 4 independent parts. A program takes and returns all parts, laid end to end along the dimension named above; an argument that names none is the same for every part.
All inputs are finite; a program needn't handle non-finite values.
Results may differ from a plain program's by a relative error of at most 0.02.
Values are sent between devices in bfloat16 or wider.
A program may use at most 768 MiB of HBM per device.

v0:
```python
import jax
import jax.numpy as jnp
from jax import lax
from jax.sharding import PartitionSpec as P

NAMES = ("w_gate", "w_up", "w_down")


def matmul(a, w):
    return jnp.dot(a, w, preferred_element_type=jnp.float32).astype(jnp.bfloat16)


def normed(h):
    wide = h.astype(jnp.float32)
    scale = lax.rsqrt(jnp.mean(wide**2, -1, keepdims=True) + 1e-6)
    return (wide * scale).astype(jnp.bfloat16)


def layer(h, w):
    a = normed(h)
    gate = jnp.dot(a, w["w_gate"], preferred_element_type=jnp.float32)
    up = jnp.dot(a, w["w_up"], preferred_element_type=jnp.float32)
    return h + matmul((jax.nn.silu(gate) * up).astype(jnp.bfloat16), w["w_down"])


def adamw(w, m, v, g):
    m = 0.9 * m + 0.1 * g
    v = 0.95 * v + 0.05 * g * g
    step = m * lax.rsqrt(v + 1e-8) + 0.1 * w
    return (w - 0.02 * step).astype(jnp.bfloat16), m, v


def solution(mesh):
    def fetched(weights, number):
        return {name: lax.all_gather(w[number], "dp", axis=0, tiled=True) for name, w in zip(NAMES, weights, strict=True)}

    def step(x, dy, *arrays):
        weights, m, v = (arrays[i : i + 3] for i in (0, 3, 6))
        layers = weights[0].shape[0]
        h, kept = x[0], []
        for number in range(layers):
            kept.append(h)
            h = layer(h, fetched(weights, number))
        by_h, mine = dy[0], [None] * layers
        for number in reversed(range(layers)):
            _, back = jax.vjp(lambda w, h: layer(h, w), fetched(weights, number), kept[number])
            by_w, by_h = back(by_h)
            mine[number] = [lax.psum_scatter(by_w[name], "dp", scatter_dimension=0, tiled=True) for name in NAMES]
        gradients = [jnp.stack([mine[number][i] for number in range(layers)]).astype(jnp.float32) for i in range(3)]
        new = [adamw(w.astype(jnp.float32), m, v, g) for w, m, v, g in zip(weights, m, v, gradients, strict=True)]
        return tuple(one[which] for which in range(3) for one in new)

    states, cut = P(("rep", "dp"), None, None), P(None, "dp", None)
    return jax.shard_map(
        step,
        mesh=mesh,
        in_specs=(states, states) + (cut,) * 9,
        out_specs=(P("rep", "dp", None),) * 9,
        check_vma=False,
    )
```

profile of v0, /device:TPU:112, one launch (start us, length us, event | category | flops | bytes accessed | tf_op | source)
XLA Modules:
  0.0 1216.6 jit_solution(15773976665678340799)
XLA Ops:
  7.3 4.7 fusion.97
  12.0 0.1 all-gather.15.cloned.1.call-start
  12.1 4.7 fusion.96
  16.8 0.1 all-gather.17.cloned.1.call-start
  16.9 4.7 fusion.95
  21.7 0.6 all-gather.23.cloned.1.call-update
  22.3 0.6 all-gather.21.cloned.1.call-update
  23.0 0.6 all-gather.19.cloned.1.call-update
  23.6 7.9 copy.20
  31.5 3.6 fusion.19
  35.1 7.9 copy.21
  43.0 55.2 %all-gather.13.cloned.1.call-done = bf16[1,1280,3456]{2,1,0:T(8,128)(2,1)} async-done(((bf16[1,320,3456]{2,1,0:T(8,128)(2,1)}), bf16[1,1280,3456]{2,1,0:T(8,128)(2,1)}) %all-gather.13.cloned.1.call-update) | async-done | bytes 8847376 | tf_op jit(solution)/shard_map/all_gather | solution.py:35
  98.2 26.8 %fusion.54 = f32[2048,3456]{1,0:T(8,128)} fusion(bf16[1,1280,3456]{2,1,0:T(8,128)(2,1)} %all-gather.13.cloned.1.call-done, bf16[1,2048,1280]{1,2,0:T(8,128)(2,1)} %copy.20, f32[2048]{0:T(1024)S(1)} %add_rsqrt_fusion), kind=kOutput, calls=%fused_computation.85 | convolution fusion | flops 18127257600 | bytes 42409984 | tf_op jit(solution)/shard_map/dot_general | solution.py:21
  125.0 59.4 %all-gather.15.cloned.1.call-done = bf16[1,1280,3456]{2,1,0:T(8,128)(2,1)} async-done(((bf16[1,320,3456]{2,1,0:T(8,128)(2,1)}), bf16[1,1280,3456]{2,1,0:T(8,128)(2,1)}) %all-gather.15.cloned.1.call-update) | async-done | bytes 8847376 | tf_op jit(solution)/shard_map/all_gather | solution.py:35
  184.4 35.5 %multiply_convert_fusion.1 = (bf16[2048,3456]{1,0:T(8,128)(2,1)}, f32[2048,3456]{1,0:T(8,128)}) fusion(f32[2048,3456]{1,0:T(8,128)} %fusion.54, bf16[1,1280,3456]{2,1,0:T(8,128)(2,1)} %all-gather.15.cloned.1.call-done, bf16[1,2048,1280]{1,2,0:T(8,128)(2,1)} %copy.20, f32[2048]{0:T(1024)S(1)} %add_rsqrt_fusion), kind=kOutput, calls=%fused_computation.17 | convolution fusion | flops 18169724928 | bytes 84877312 | tf_op jit(solution)/shard_map/dot_general | solution.py:22
  219.9 50.8 %all-gather.17.cloned.1.call-done = bf16[1,3456,1280]{2,1,0:T(8,128)(2,1)} async-done(((bf16[1,864,1280]{2,1,0:T(8,128)(2,1)}), bf16[1,3456,1280]{2,1,0:T(8,128)(2,1)}) %all-gather.17.cloned.1.call-update) | async-done | bytes 8847376 | tf_op jit(solution)/shard_map/all_gather | solution.py:35
  270.6 26.7 %fusion.23 = (f32[2048]{0:T(1024)S(1)}, bf16[2048,1280]{0,1:T(8,128)(2,1)}) fusion(bf16[2048,3456]{1,0:T(8,128)(2,1)} %get-tuple-element.24, bf16[1,3456,1280]{2,1,0:T(8,128)(2,1)} %all-gather.17.cloned.1.call-done, bf16[1,2048,1280]{1,2,0:T(8,128)(2,1)} %copy.20), kind=kOutput, calls=%fused_computation.54 | convolution fusion | flops 18132498432 | bytes 33497088 | tf_op jit(solution)/shard_map/dot_general | solution.py:10
  297.3 0.6 copy-done.3
  297.9 58.8 %all-gather.23.cloned.1.call-done = bf16[1,1280,3456]{2,1,0:T(8,128)(2,1)} async-done(((bf16[1,320,3456]{2,1,0:T(8,128)(2,1)}), bf16[1,1280,3456]{2,1,0:T(8,128)(2,1)}) %all-gather.23.cloned.1.call-update) | async-done | bytes 8847376 | tf_op jit(solution)/shard_map/all_gather | solution.py:35
  356.7 26.8 %fusion.41 = f32[2048,3456]{1,0:T(8,128)} fusion(bf16[1,1280,3456]{2,1,0:T(8,128)(2,1)} %all-gather.23.cloned.1.call-done, bf16[2048,1280]{0,1:T(8,128)(2,1)} %get-tuple-element.27, f32[2048]{0:T(1024)S(1)} %fusion.83), kind=kOutput, calls=%fused_computation.72 | convolution fusion | flops 18127257600 | bytes 42409984 | tf_op jit(solution)/shard_map/jvp()/dot_general | solution.py:22
  383.5 59.3 %all-gather.21.cloned.1.call-done = bf16[1,3456,1280]{2,1,0:T(8,128)(2,1)} async-done(((bf16[1,864,1280]{2,1,0:T(8,128)(2,1)}), bf16[1,3456,1280]{2,1,0:T(8,128)(2,1)}) %all-gather.21.cloned.1.call-update) | async-done | bytes 8847376 | tf_op jit(solution)/shard_map/all_gather | solution.py:35
  442.8 26.3 %convolution_convert_fusion.4 = bf16[2048,3456]{1,0:T(8,128)(2,1)} fusion(bf16[1,3456,1280]{2,1,0:T(8,128)(2,1)} %all-gather.21.cloned.1.call-done, bf16[1,2048,1280]{2,1,0:T(8,128)(2,1)} %param.12), kind=kOutput, calls=%fused_computation.33 | convolution fusion | flops 18126471168 | bytes 28246016 | tf_op jit(solution)/shard_map/transpose(jvp())/dot_general | solution.py:10
  469.1 59.8 %all-gather.19.cloned.1.call-done = bf16[1,1280,3456]{2,1,0:T(8,128)(2,1)} async-done(((bf16[1,320,3456]{2,1,0:T(8,128)(2,1)}), bf16[1,1280,3456]{2,1,0:T(8,128)(2,1)}) %all-gather.19.cloned.1.call-update) | async-done | bytes 8847376 | tf_op jit(solution)/shard_map/all_gather | solution.py:35
  528.8 42.9 %fusion.2 = (bf16[2048,3456]{1,0:T(8,128)(2,1)}, f32[2048,3456]{1,0:T(8,128)}) fusion(f32[2048,3456]{1,0:T(8,128)} %fusion.41, bf16[2048,3456]{1,0:T(8,128)(2,1)} %convolution_convert_fusion.4, bf16[1,1280,3456]{2,1,0:T(8,128)(2,1)} %all-gather.19.cloned.1.call-done, bf16[2048,1280]{0,1:T(8,128)(2,1)} %get-tuple-element.27, f32[2048]{0:T(1024)S(1)} %fusion.83), kind=kOutput, calls=%fused_computation.8 | convolution fusion | flops 18212192256 | bytes 99033088 | tf_op jit(solution)/shard_map/jvp()/dot_general | solution.py:21
  571.7 25.8 %fusion.59 = bf16[2048,1280]{0,1:T(8,128)(2,1)} fusion(bf16[2048,3456]{1,0:T(8,128)(2,1)} %get-tuple-element.28, bf16[1,1280,3456]{2,1,0:T(8,128)(2,1)} %all-gather.19.cloned.1.call-done), kind=kOutput, calls=%fused_computation.88 | convolution fusion | flops 18119393280 | bytes 28246016 | tf_op jit(solution)/shard_map/transpose(jvp())/dot_general | solution.py:21
  597.5 31.5 %fusion.25 = (f32[2048]{0:T(1024)S(1)}, bf16[2048,1280]{0,1:T(8,128)(2,1)}) fusion(bf16[2048,1280]{0,1:T(8,128)(2,1)S(1)} %copy-done, bf16[2048,1280]{0,1:T(8,128)(2,1)} %fusion.59, bf16[1,1280,3456]{2,1,0:T(8,128)(2,1)} %all-gather.23.cloned.1.call-done, bf16[2048,3456]{1,0:T(8,128)(2,1)} %convolution_convert_fusion.4, f32[2048,3456]{1,0:T(8,128)} %get-tuple-element.29), kind=kOutput, calls=%fused_computation.56 | convolution fusion | flops 18177587200 | bytes 67051520 | tf_op jit(solution)/shard_map/transpose(jvp())/dot_general | solution.py:22
  629.1 12.4 %fusion.71 = bf16[2048,1280]{0,1:T(8,128)(2,1)} fusion(bf16[2048,1280]{0,1:T(8,128)(2,1)} %get-tuple-element.27, bf16[2048,1280]{0,1:T(8,128)(2,1)} %get-tuple-element.31, bf16[1,2048,1280]{1,2,0:T(8,128)(2,1)} %copy.21, f32[2048]{0:T(1024)S(1)} %multiply_multiply_fusion.3, f32[2048]{0:T(1024)S(1)} %fusion.83), kind=kLoop, calls=%fused_computation.92 | loop fusion | flops 18350080 | bytes 20987904 | tf_op jit(solution)/shard_map/transpose(jvp())/add_any | solution.py:14
  641.5 25.5 %convolution_convert_fusion.3 = bf16[2048,3456]{1,0:T(8,128)(2,1)} fusion(bf16[2048,1280]{0,1:T(8,128)(2,1)} %fusion.71, bf16[1,3456,1280]{2,1,0:T(8,128)(2,1)} %all-gather.17.cloned.1.call-done), kind=kOutput, calls=%fused_computation.32 | convolution fusion | flops 18126471168 | bytes 28246016 | tf_op jit(solution)/shard_map/transpose(jvp())/dot_general | solution.py:10
  667.0 30.2 %fusion.14 = bf16[1280,3456]{1,0:T(8,128)(2,1)} fusion(bf16[2048,3456]{1,0:T(8,128)(2,1)} %convolution_convert_fusion.3, f32[2048,3456]{1,0:T(8,128)} %fusion.54, bf16[1,2048,1280]{1,2,0:T(8,128)(2,1)} %copy.20, f32[2048]{0:T(1024)S(1)} %copy-done.6), kind=kOutput, calls=%fused_computation.27 | convolution fusion | flops 18174148608 | bytes 56565760 | tf_op jit(solution)/shard_map/transpose(jvp())/dot_general | solution.py:22
  697.2 0.1 reduce-scatter.13.cloned.1.call-start
  697.3 30.4 %fusion.13 = bf16[1280,3456]{1,0:T(8,128)(2,1)} fusion(bf16[2048,3456]{1,0:T(8,128)(2,1)} %convolution_convert_fusion.4, bf16[2048,1280]{0,1:T(8,128)(2,1)} %get-tuple-element.27, f32[2048]{0:T(1024)S(1)} %fusion.83, f32[2048,3456]{1,0:T(8,128)} %get-tuple-element.29), kind=kOutput, calls=%fused_computation.26 | convolution fusion | flops 18174148608 | bytes 56565760 | tf_op jit(solution)/shard_map/transpose(jvp())/dot_general | solution.py:22
  727.8 0.1 reduce-scatter.17.cloned.1.call-start
  727.9 31.3 %convolution_convert_fusion.1 = bf16[3456,1280]{1,0:T(8,128)(2,1)} fusion(f32[2048,3456]{1,0:T(8,128)} %fusion.41, bf16[1,2048,1280]{2,1,0:T(8,128)(2,1)} %param.12, f32[2048,3456]{1,0:T(8,128)} %get-tuple-element.29), kind=kOutput, calls=%fused_computation.30 | convolution fusion | flops 18166284288 | bytes 70713344 | tf_op jit(solution)/shard_map/transpose(jvp())/dot_general | solution.py:10
  759.3 0.1 reduce-scatter.15.cloned.1.call-start
  759.4 24.9 %convolution_convert_fusion.2 = bf16[3456,1280]{1,0:T(8,128)(2,1)} fusion(bf16[2048,3456]{1,0:T(8,128)(2,1)} %get-tuple-element.24, bf16[2048,1280]{0,1:T(8,128)(2,1)} %fusion.71), kind=kOutput, calls=%fused_computation.31 | convolution fusion | flops 18123816960 | bytes 28246016 | tf_op jit(solution)/shard_map/transpose(jvp())/dot_general | solution.py:10
  784.4 0.6 copy-done.7
  785.0 34.5 %fusion.15 = bf16[1280,3456]{1,0:T(8,128)(2,1)} fusion(f32[2048,3456]{1,0:T(8,128)} %fusion.54, f32[2048,3456]{1,0:T(8,128)} %get-tuple-element.25, bf16[2048,3456]{1,0:T(8,128)(2,1)} %convolution_convert_fusion.3, bf16[1,2048,1280]{1,2,0:T(8,128)(2,1)} %copy.20, f32[2048]{0:T(1024)S(1)} %copy-done.7), kind=kOutput, calls=%fused_computation.29 | convolution fusion | flops 18209538048 | bytes 84877312 | tf_op jit(solution)/shard_map/transpose(jvp())/dot_general | solution.py:21
  819.5 0.1 reduce-scatter.9.cloned.1.call-start
  819.6 0.6 copy-done.2
  820.2 26.8 %convolution_convert_fusion = bf16[1280,3456]{1,0:T(8,128)(2,1)} fusion(bf16[2048,3456]{1,0:T(8,128)(2,1)} %get-tuple-element.28, bf16[2048,1280]{0,1:T(8,128)(2,1)} %get-tuple-element.27, f32[2048]{0:T(1024)S(1)} %copy-done.2), kind=kOutput, calls=%fused_computation.28 | convolution fusion | flops 18127257600 | bytes 28254208 | tf_op jit(solution)/shard_map/transpose(jvp())/dot_general | solution.py:21
  847.0 14.4 %reduce-scatter.13.cloned.1.call-done = bf16[320,3456]{1,0:T(8,128)(2,1)} async-done(((bf16[1280,3456]{1,0:T(8,128)(2,1)}), bf16[320,3456]{1,0:T(8,128)(2,1)}) %reduce-scatter.13.cloned.1.call-update) | async-done | bytes 2211856 | tf_op jit(solution)/shard_map/reduce_scatter | solution.py:48
  861.4 17.8 %fusion.32 = (bf16[2,320,3456]{2,1,0:T(8,128)(2,1)}, f32[2,320,3456]{2,1,0:T(8,128)}, f32[2,320,3456]{2,1,0:T(8,128)}) fusion(bf16[2,320,3456]{2,1,0:T(8,128)(2,1)} %param.14, bf16[1,320,3456]{2,1,0:T(8,128)(2,1)} %bitcast.73, bf16[1,320,3456]{2,1,0:T(8,128)(2,1)} %bitcast.72, f32[2,320,3456]{2,1,0:T(8,128)} %param.20, f32[2,320,3456]{2,1,0:T(8,128)} %param.17), kind=kLoop, calls=%fused_computation.63 | loop fusion | flops 42024960 | bytes 48660480 | tf_op jit(solution)/shard_map/convert_element_type | solution.py:30
  879.2 64.5 %reduce-scatter.17.cloned.1.call-done = bf16[864,1280]{1,0:T(8,128)(2,1)} async-done(((bf16[3456,1280]{1,0:T(8,128)(2,1)}), bf16[864,1280]{1,0:T(8,128)(2,1)}) %reduce-scatter.17.cloned.1.call-update) | async-done | bytes 2211856 | tf_op jit(solution)/shard_map/reduce_scatter | solution.py:48
  943.7 82.1 %reduce-scatter.15.cloned.1.call-done = bf16[864,1280]{1,0:T(8,128)(2,1)} async-done(((bf16[3456,1280]{1,0:T(8,128)(2,1)}), bf16[864,1280]{1,0:T(8,128)(2,1)}) %reduce-scatter.15.cloned.1.call-update) | async-done | bytes 2211856 | tf_op jit(solution)/shard_map/reduce_scatter | solution.py:48
  1025.8 18.7 %fusion.36 = (bf16[2,864,1280]{2,1,0:T(8,128)(2,1)}, f32[2,864,1280]{2,1,0:T(8,128)}, f32[2,864,1280]{2,1,0:T(8,128)}) fusion(bf16[2,864,1280]{2,1,0:T(8,128)(2,1)} %param.15, bf16[1,864,1280]{2,1,0:T(8,128)(2,1)} %bitcast.74, bf16[1,864,1280]{2,1,0:T(8,128)(2,1)} %bitcast.75, f32[2,864,1280]{2,1,0:T(8,128)} %param.21, f32[2,864,1280]{2,1,0:T(8,128)} %param.18), kind=kLoop, calls=%fused_computation.67 | loop fusion | flops 42024960 | bytes 48660480 | tf_op jit(solution)/shard_map/convert_element_type | solution.py:30
  1044.5 64.2 %reduce-scatter.7.cloned.1.call-done = bf16[320,3456]{1,0:T(8,128)(2,1)} async-done(((bf16[1280,3456]{1,0:T(8,128)(2,1)}), bf16[320,3456]{1,0:T(8,128)(2,1)}) %reduce-scatter.7.cloned.1.call-update) | async-done | bytes 2211856 | tf_op jit(solution)/shard_map/reduce_scatter | solution.py:48
  1108.7 82.7 %reduce-scatter.9.cloned.1.call-done = bf16[320,3456]{1,0:T(8,128)(2,1)} async-done(((bf16[1280,3456]{1,0:T(8,128)(2,1)}), bf16[320,3456]{1,0:T(8,128)(2,1)}) %reduce-scatter.9.cloned.1.call-update) | async-done | bytes 2211856 | tf_op jit(solution)/shard_map/reduce_scatter | solution.py:48
  1191.4 17.8 %fusion.28 = (bf16[2,320,3456]{2,1,0:T(8,128)(2,1)}, f32[2,320,3456]{2,1,0:T(8,128)}, f32[2,320,3456]{2,1,0:T(8,128)}) fusion(bf16[2,320,3456]{2,1,0:T(8,128)(2,1)} %param.13, bf16[1,320,3456]{2,1,0:T(8,128)(2,1)} %bitcast.77, bf16[1,320,3456]{2,1,0:T(8,128)(2,1)} %bitcast.76, f32[2,320,3456]{2,1,0:T(8,128)} %param.19, f32[2,320,3456]{2,1,0:T(8,128)} %param.16), kind=kLoop, calls=%fused_computation.59 | loop fusion | flops 42024960 | bytes 48660480 | tf_op jit(solution)/shard_map/convert_element_type | solution.py:30
  (32 shorter events, 0.9 us)
Async XLA Ops:
  7.2 91.0 %all-gather.13.cloned.1.call-start = ((), (), s32[]{:S(2)}) async-start(), calls=%async_computation.12 | async-start | bytes 11059200 | tf_op jit(solution)/shard_map/all_gather | solution.py:35
  12.0 172.4 %all-gather.15.cloned.1.call-start = ((), (), s32[]{:S(2)}) async-start(), calls=%async_computation.13 | async-start | bytes 11059200 | tf_op jit(solution)/shard_map/all_gather | solution.py:35
  16.8 253.8 %all-gather.17.cloned.1.call-start = ((), (), s32[]{:S(2)}) async-start(), calls=%async_computation.14 | async-start | bytes 11059200 | tf_op jit(solution)/shard_map/all_gather | solution.py:35
  21.6 335.1 %all-gather.23.cloned.1.call-start = ((), (), s32[]{:S(2)}) async-start(), calls=%async_computation.17 | async-start | bytes 11059200 | tf_op jit(solution)/shard_map/all_gather | solution.py:35
  22.2 420.5 %all-gather.21.cloned.1.call-start = ((), (), s32[]{:S(2)}) async-start(), calls=%async_computation.16 | async-start | bytes 11059200 | tf_op jit(solution)/shard_map/all_gather | solution.py:35
  22.9 506.0 %all-gather.19.cloned.1.call-start = ((), (), s32[]{:S(2)}) async-start(), calls=%async_computation.15 | async-start | bytes 11059200 | tf_op jit(solution)/shard_map/all_gather | solution.py:35
  23.5 823.5 %reduce-scatter.11.cloned.1.call-start = ((), (), s32[]{:S(2)}) async-start(), calls=%async_computation.8 | async-start | bytes 11059200 | tf_op jit(solution)/shard_map/reduce_scatter | solution.py:48
  35.1 149.3 %copy-start.5 = (f32[2048]{0:T(1024)}, f32[2048]{0:T(1024)S(1)}, u32[]{:S(2)}) copy-start(f32[2048]{0:T(1024)S(1)} %add_rsqrt_fusion) | copy-start | bytes 24580
  297.3 0.6 copy-start.3
  297.9 399.4 %copy-start.1 = (f32[2048]{0:T(1024)}, f32[2048]{0:T(1024)S(1)}, u32[]{:S(2)}) copy-start(f32[2048]{0:T(1024)S(1)} %fusion.83) | copy-start | bytes 24580
  571.7 25.8 %copy-start = (bf16[2048,1280]{0,1:T(8,128)(2,1)S(1)}, bf16[2048,1280]{0,1:T(8,128)(2,1)}, u32[]{:S(2)}) copy-start(bf16[2048,1280]{0,1:T(8,128)(2,1)} %get-tuple-element.27) | copy-start | bytes 15728644
  597.5 31.5 %copy-start.4 = (f32[2048]{0:T(1024)S(1)}, f32[2048]{0:T(1024)}, u32[]{:S(2)}) copy-start(f32[2048]{0:T(1024)} %copy-done.3) | copy-start | bytes 24580
  641.5 25.5 %copy-start.6 = (f32[2048]{0:T(1024)S(1)}, f32[2048]{0:T(1024)}, u32[]{:S(2)}) copy-start(f32[2048]{0:T(1024)} %copy-done.5) | copy-start | bytes 24580
  697.2 164.1 %reduce-scatter.13.cloned.1.call-start = ((), (), s32[]{:S(2)}) async-start(), calls=%async_computation.9 | async-start | bytes 11059200 | tf_op jit(solution)/shard_map/reduce_scatter | solution.py:48
  727.8 215.9 %reduce-scatter.17.cloned.1.call-start = ((), (), s32[]{:S(2)}) async-start(), calls=%async_computation.11 | async-start | bytes 11059200 | tf_op jit(solution)/shard_map/reduce_scatter | solution.py:48
  759.3 266.5 %reduce-scatter.15.cloned.1.call-start = ((), (), s32[]{:S(2)}) async-start(), calls=%async_computation.10 | async-start | bytes 11059200 | tf_op jit(solution)/shard_map/reduce_scatter | solution.py:48
  784.3 0.7 copy-start.7
  784.3 324.4 %reduce-scatter.7.cloned.1.call-start = ((), (), s32[]{:S(2)}) async-start(), calls=%async_computation.6 | async-start | bytes 11059200 | tf_op jit(solution)/shard_map/reduce_scatter | solution.py:48
  819.5 0.7 copy-start.2
  819.5 371.9 %reduce-scatter.9.cloned.1.call-start = ((), (), s32[]{:S(2)}) async-start(), calls=%async_computation.7 | async-start | bytes 11059200 | tf_op jit(solution)/shard_map/reduce_scatter | solution.py:48
Sparse Core Ops, SparseCore 0:
  12.1 86.0 all-gather.12
  100.3 84.0 all-gather.14
  186.5 84.0 all-gather.16
  272.6 84.0 all-gather.22
  358.7 84.0 all-gather.20
  444.7 84.0 all-gather.18
  697.4 81.1 reduce-scatter.10
  781.5 79.8 reduce-scatter.12
  863.8 79.8 reduce-scatter.16
  945.9 79.8 reduce-scatter.14
  1028.8 79.8 reduce-scatter.6
  1111.5 79.8 reduce-scatter.8
where the time goes:
time: 1230 us; the launch traced here: 1220 us
  waiting for transfers between devices  653 us (53%)
  matrix products  446 us (36%)
  other arithmetic  70.3 us (6%)
  local copies, waits for them, and re-layouts  31.5 us (3%)
  between operations  14.8 us (1%)
    all_gather x6, waiting for transfers between devices, fetched(): lax.all_gather(w[number], 'dp', axis=0, tiled=True)  343 us
    reduce_scatter x6, waiting for transfers between devices, step(): lax.psum_scatter(by_w[name], 'dp', scatter_dimension=0, tiled=True)  308 us
    dot_general x5, matrix products, layer(): gate = jnp.dot(a, w['w_gate'], preferred_element_type=jnp.float32)  157 us
    dot_general x5, matrix products, layer(): up = jnp.dot(a, w['w_up'], preferred_element_type=jnp.float32)  154 us
    dot_general x5, matrix products, matmul(): jnp.dot(a, w, preferred_element_type=jnp.float32).astype(jnp.bfloat16)  135 us
    convert_element_type x3, other arithmetic, adamw(): return ((w - 0.02 * step).astype(jnp.bfloat16), m, v)  54.3 us
  transfers between devices with their start and end apart: 12, of which 11 were waited for; matrix products, arithmetic and copies ran while one was open for 29% of the time, Pallas kernels for 0%

commit v1 on v0

v1 whole, which is shorter than its diff:
```python
import jax
import jax.numpy as jnp
from jax import lax
from jax.experimental import pallas as pl
from jax.experimental.pallas import tpu as pltpu
from jax.sharding import PartitionSpec as P


BF, F32 = jnp.bfloat16, jnp.float32
MESH = pl.DeviceIdType.MESH
ROWS = 256
GU_CUTS, DOWN_CUTS, GRAD_CUTS = 3, 2, 9


def dot(a, b, ca, cb):
    return lax.dot_general(a, b, (((ca,), (cb,)), ((), ())), preferred_element_type=F32)


def normed(h):
    wide = h.astype(F32)
    scale = lax.rsqrt(jnp.mean(wide**2, -1, keepdims=True) + 1e-6)
    return (wide * scale).astype(BF)


def gated(gate, up):
    return (jax.nn.silu(gate) * up).astype(BF)


def adamw(w, m, v, g):
    m = 0.9 * m + 0.1 * g
    v = 0.95 * v + 0.05 * g * g
    step = m * lax.rsqrt(v + 1e-8) + 0.1 * w
    return (w - 0.02 * step).astype(BF), m, v


def forward_kernel(n, x_ref, dy_ref, wg, wu, wd, *refs):
    (g0, u0, d0, g1, u1, d1, gate0, up0, gate1, up1, z0, h1, by_d1,
     zbuf, abuf, xbuf, hbuf, wbuf, dbuf, gst, ust, ost, send, recv, lsem, ssem, osem) = refs
    whole = ((g0, u0, d0), (g1, u1, d1))
    tokens, d = abuf.shape
    ff = zbuf.shape[1]
    fc, dc, gc = ff // GU_CUTS, d // DOWN_CUTS, ff // GRAD_CUTS
    steps = tokens // ROWS
    me = lax.axis_index("dp")
    rep = lax.axis_index("rep")
    core = lax.rem(rep, 2)
    left, right, across = lax.rem(me + n - 1, n), lax.rem(me + 1, n), lax.rem(me + 2, n)
    to_left, to_right, to_other = {"dp": left}, {"dp": right}, {"rep": rep + 1 - 2 * core}

    units = [(layer, kind, j) for layer in range(2) for kind, cuts in (("gu", GU_CUTS), ("d", DOWN_CUTS)) for j in range(cuts)]

    def parts(unit):
        layer, kind, j = units[unit]
        if kind == "gu":
            cols = pl.ds(j * fc, fc)
            return [(whole[layer][0], wg.at[layer], cols), (whole[layer][1], wu.at[layer], cols)]
        return [(whole[layer][2], wd.at[layer], pl.ds(j * dc, dc))]

    def at(start, size):
        return pl.ds(pl.multiple_of(start, 16), size)

    def copies(unit):
        out = []
        for p, (w, block, cols) in enumerate(parts(unit)):
            rows = block.shape[0]
            half = rows // 2
            a = (half // 2 + 15) // 16 * 16
            s = core * half

            def move(k, src, dst, to, p=p):
                return pltpu.make_async_remote_copy(
                    src_ref=src, dst_ref=dst, send_sem=send.at[unit, p, k], recv_sem=recv.at[unit, p, k], device_id=to, device_id_type=MESH
                )

            mine, here = block.at[at(s, half), cols], w.at[at(me * rows + s, half), cols]
            first, second = w.at[at(left * rows + s, a), cols], w.at[at(right * rows + s + a, half - a), cols]
            trade = [w.at[at(b * rows + s, half), cols] for b in (left, right, across)]
            out.append(
                [move(0, mine, here, to_right), move(1, mine, here, to_left), move(2, first, first, to_right), move(3, second, second, to_left)]
                + [move(4 + i, t, t, to_other) for i, t in enumerate(trade)]
            )
        return out

    def A(unit):
        for c in copies(unit):
            c[0].start()
            c[1].start()

    def B(unit):
        for c in copies(unit):
            c[0].wait_recv()
            c[2].start()
            c[1].wait_recv()
            c[3].start()
        for c in copies(unit):
            c[4].start()
            c[5].start()

    def C(unit):
        for c in copies(unit):
            c[2].wait_recv()
            c[3].wait_recv()
            c[6].start()

    def D(unit):
        for c in copies(unit):
            for k in (4, 5, 6):
                c[k].wait_recv()

    stay = []
    for layer in range(2):
        for i, w in enumerate((wg, wu)):
            rows = w.shape[1]
            stay.append((w.at[layer], zbuf.at[pl.ds((2 * layer + i) * rows, rows)], whole[layer][i].at[at(me * rows, rows)]))
        rows = wd.shape[1]
        stay.append((wd.at[layer], hbuf.at[pl.ds(layer * rows, rows)], whole[layer][2].at[at(me * rows, rows)]))

    barrier = pltpu.get_barrier_semaphore()
    for to in (to_left, to_right, to_other):
        pl.semaphore_signal(barrier, inc=1, device_id=to, device_id_type=MESH)
    pl.semaphore_wait(barrier, 3)

    A(0)
    take = pltpu.make_async_copy(x_ref, xbuf, lsem.at[6])
    take.start()
    ins = [pltpu.make_async_copy(src, mid, lsem.at[i]) for i, (src, mid, _) in enumerate(stay)]
    outs = [pltpu.make_async_copy(mid, dst, lsem.at[i]) for i, (_, mid, dst) in enumerate(stay)]
    for c in ins:
        c.start()
    for i, c in enumerate(ins):
        c.wait()
        outs[i].start()
    take.wait()

    def norm(src):
        @pl.loop(0, steps)
        def _(i):
            rows = pl.ds(pl.multiple_of(i * ROWS, ROWS), ROWS)
            abuf[rows, :] = normed(src[rows, :])

    norm(xbuf)
    for c in outs:
        c.wait()
    B(0)
    A(1)

    def ready(unit):
        C(unit)
        D(unit)

    def hook(unit):
        B(unit + 1)
        if unit + 2 < len(units):
            A(unit + 2)

    def gate_up(layer, gate, up, base):
        wgate, wup, _ = whole[layer]

        @pl.loop(0, GU_CUTS)
        def _(j):
            for jj in range(GU_CUTS):
                pl.when(j == jj)(lambda u=base + jj: ready(u))
            cols = pl.ds(pl.multiple_of(j * fc, 128), fc)
            ga = pltpu.make_async_copy(wgate.at[:, cols], wbuf.at[0], lsem.at[0])
            ua = pltpu.make_async_copy(wup.at[:, cols], wbuf.at[1], lsem.at[1])
            ga.start()
            ua.start()
            ga.wait()
            ua.wait()

            @pl.loop(0, steps)
            def _(i):
                for jj in range(GU_CUTS):
                    pl.when((j == jj) & (i == steps - 2))(lambda u=base + jj: hook(u))
                rows = pl.ds(pl.multiple_of(i * ROWS, ROWS), ROWS)
                slot = lax.rem(i, 2)
                put_g = pltpu.make_async_copy(gst.at[slot], gate.at[rows, cols], ssem.at[0, slot])
                put_u = pltpu.make_async_copy(ust.at[slot], up.at[rows, cols], ssem.at[1, slot])

                @pl.when(i >= 2)
                def _():
                    put_g.wait()
                    put_u.wait()

                g = dot(abuf[rows, :], wbuf[0], 1, 0)
                u = dot(abuf[rows, :], wbuf[1], 1, 0)
                gst[slot] = g
                ust[slot] = u
                zbuf[rows, cols] = gated(g, u)
                put_g.start()
                put_u.start()

            for slot in range(2):
                rows = pl.ds(slot * ROWS, ROWS)
                pltpu.make_async_copy(gst.at[slot], gate.at[rows, cols], ssem.at[0, slot]).wait()
                pltpu.make_async_copy(ust.at[slot], up.at[rows, cols], ssem.at[1, slot]).wait()

    gate_up(0, gate0, up0, 0)
    put_z = pltpu.make_async_copy(zbuf, z0, lsem.at[2])
    put_z.start()

    @pl.loop(0, DOWN_CUTS)
    def _(j):
        for jj in range(DOWN_CUTS):
            pl.when(j == jj)(lambda u=GU_CUTS + jj: ready(u))
        cols = pl.ds(pl.multiple_of(j * dc, 128), dc)
        da = pltpu.make_async_copy(d0.at[:, cols], dbuf, lsem.at[0])
        da.start()
        da.wait()

        @pl.loop(0, steps)
        def _(i):
            for jj in range(DOWN_CUTS):
                pl.when((j == jj) & (i == steps - 2))(lambda u=GU_CUTS + jj: hook(u))
            rows = pl.ds(pl.multiple_of(i * ROWS, ROWS), ROWS)
            hbuf[rows, cols] = xbuf[rows, cols] + dot(zbuf[rows, :], dbuf[...], 1, 0).astype(BF)

    put_h = pltpu.make_async_copy(hbuf, h1, lsem.at[3])
    put_h.start()
    take = pltpu.make_async_copy(dy_ref, xbuf, lsem.at[6])
    take.start()
    norm(hbuf)
    put_z.wait()
    gate_up(1, gate1, up1, GU_CUTS + DOWN_CUTS)
    take.wait()
    last = len(units) - 1

    @pl.loop(0, GRAD_CUTS)
    def _(t):
        pl.when(t == 2)(lambda: B(last))
        pl.when(t == 5)(lambda: C(last - 1))
        cols = pl.ds(pl.multiple_of(t * gc, 128), gc)
        slot = lax.rem(t, 2)
        put = pltpu.make_async_copy(ost.at[slot], by_d1.at[pl.ds(pl.multiple_of(t * gc, 128), gc)], osem.at[slot])
        pl.when(t >= 2)(lambda: put.wait())
        ost[slot] = dot(zbuf[:, cols], xbuf[...], 0, 0).astype(BF)
        put.start()

    for slot in range(2):
        pltpu.make_async_copy(ost.at[slot], by_d1.at[pl.ds(slot * gc, gc)], osem.at[slot]).wait()
    D(last - 1)
    C(last)
    D(last)
    put_h.wait()
    for unit in range(len(units)):
        for c in copies(unit):
            for one in c:
                one.wait_send()


def forward(n, x, dy, wg, wu, wd):
    tokens, d = x.shape
    layers, _, ff = wg.shape
    fc, dc, gc = ff // GU_CUTS, d // DOWN_CUTS, ff // GRAD_CUTS
    n_units = layers * (GU_CUTS + DOWN_CUTS)
    out = lambda *shape, dtype=BF: jax.ShapeDtypeStruct(shape, dtype)
    layer = [out(d, ff), out(d, ff), out(ff, d)]
    pre = [out(tokens, ff, dtype=F32)] * 4
    flops = 2 * tokens * d * ff * 6
    return pl.pallas_call(
        lambda *refs: forward_kernel(n, *refs),
        out_shape=layer + layer + pre + [out(tokens, ff), out(tokens, d), out(ff, d)],
        in_specs=[pl.BlockSpec(memory_space=pl.ANY)] * 5,
        out_specs=[pl.BlockSpec(memory_space=pl.ANY)] * 13,
        scratch_shapes=[
            pltpu.VMEM((tokens, ff), BF),
            pltpu.VMEM((tokens, d), BF),
            pltpu.VMEM((tokens, d), BF),
            pltpu.VMEM((tokens, d), BF),
            pltpu.VMEM((2, d, fc), BF),
            pltpu.VMEM((ff, dc), BF),
            pltpu.VMEM((2, ROWS, fc), F32),
            pltpu.VMEM((2, ROWS, fc), F32),
            pltpu.VMEM((2, gc, d), BF),
            pltpu.SemaphoreType.DMA((n_units, 2, 7)),
            pltpu.SemaphoreType.DMA((n_units, 2, 7)),
            pltpu.SemaphoreType.DMA((7,)),
            pltpu.SemaphoreType.DMA((2, 2)),
            pltpu.SemaphoreType.DMA((2,)),
        ],
        compiler_params=pltpu.CompilerParams(collective_id=0, has_side_effects=True, vmem_limit_bytes=67043328),
        cost_estimate=pl.CostEstimate(flops=flops, bytes_accessed=300_000_000, transcendentals=0),
        name="gather_forward",
    )(x, dy, wg, wu, wd)


def solution(mesh):
    n = mesh.shape["dp"]

    def scattered(g):
        return lax.psum_scatter(g, "dp", scatter_dimension=0, tiled=True)

    def step(x, dy, *arrays):
        weights, m, v = (arrays[i : i + 3] for i in (0, 3, 6))
        x, dy = x[0], dy[0]
        _, _, d0, g1, u1, d1, gate0, up0, gate1, up1, z0, h1, by_d1 = forward(n, x, dy, *weights)
        sum_d1 = scattered(by_d1)
        a0 = normed(x)
        a1, back_a1 = jax.vjp(normed, h1)

        by_z1 = dot(dy, d1, 1, 1).astype(BF)
        by_gate1, by_up1 = (t.astype(BF) for t in jax.vjp(gated, gate1, up1)[1](by_z1))
        by_g1 = dot(a1, by_gate1, 0, 0).astype(BF)
        sum_g1 = scattered(by_g1)
        by_u1 = dot(a1, by_up1, 0, 0).astype(BF)
        by_u1, by_g1, by_gate1, by_up1 = lax.optimization_barrier((by_u1, by_g1, by_gate1, by_up1))
        sum_u1 = scattered(by_u1)
        by_a1 = dot(by_gate1, g1, 1, 1).astype(BF) + dot(by_up1, u1, 1, 1).astype(BF)
        by_h1 = dy + back_a1(by_a1)[0]
        by_d0 = dot(z0, by_h1, 0, 0).astype(BF)
        sum_d0 = scattered(by_d0)
        by_z0 = dot(by_h1, d0, 1, 1).astype(BF)
        by_gate0, by_up0 = (t.astype(BF) for t in jax.vjp(gated, gate0, up0)[1](by_z0))
        sum_g0 = scattered(dot(a0, by_gate0, 0, 0).astype(BF))
        sum_u0 = scattered(dot(a0, by_up0, 0, 0).astype(BF))

        gradients = [jnp.stack(pair).astype(F32) for pair in ((sum_g0, sum_g1), (sum_u0, sum_u1), (sum_d0, sum_d1))]
        new = [adamw(w.astype(F32), m, v, g) for w, m, v, g in zip(weights, m, v, gradients, strict=True)]
        return tuple(one[which] for which in range(3) for one in new)

    states, cut = P(("rep", "dp"), None, None), P(None, "dp", None)
    return jax.shard_map(
        step,
        mesh=mesh,
        in_specs=(states, states) + (cut,) * 9,
        out_specs=(P("rep", "dp", None),) * 9,
        check_vma=False,
    )
```

time: 1230 us -> 1020 us (0.83)
  Pallas kernels: 0 us -> 267 us
  waiting for transfers between devices: 653 us -> 395 us
  matrix products: 446 us -> 265 us
  local copies, waits for them, and re-layouts: 31.5 us -> 0.61 us
    all_gather x6 -> x0, waiting for transfers between devices: 343 us -> none  [fetched(): lax.all_gather(w[number], 'dp', axis=0, tiled=True)]
    pallas_call x0 -> x1, Pallas kernels: none -> 267 us  [forward(): pl.pallas_call(lambda *refs: forward_kernel(n, *refs), out_shape=layer +...]
    dot_general x15 -> x9, matrix products: 446 us -> 265 us  [dot(): lax.dot_general(a, b, (((ca,), (cb,)), ((), ())), preferred_element_type=...]
    reduce_scatter x6, waiting for transfers between devices: 308 us -> 393 us  [scattered(): return lax.psum_scatter(g, 'dp', scatter_dimension=0, tiled=True)]
    unnamed x18 -> x10, local copies, waits for them, and re-layouts: 17.5 us -> 0.61 us
    slice x3 -> x0, local copies, waits for them, and re-layouts: 14 us -> none  [fetched(): w[number]]
    add_any x1 -> x0, other arithmetic: 12.4 us -> none  [normed(): wide = h.astype(jnp.float32)]
  transfers between devices with their start and end apart: 12 -> 6, of which waited for: 11 -> 6; matrix products, arithmetic and copies ran while one was open for 29% -> 10% of each run, Pallas kernels for 0% -> 0%
where the time goes in v1:
time: 1020 us; the launch traced here: 1010 us
  waiting for transfers between devices  395 us (39%)
  Pallas kernels  267 us (26%)
  matrix products  265 us (26%)
  other arithmetic  71 us (7%)
  between operations  14.8 us (1%)
    reduce_scatter x6, waiting for transfers between devices, scattered(): return lax.psum_scatter(g, 'dp', scatter_dimension=0, tiled=True)  393 us
    pallas_call x1, Pallas kernels, forward(): pl.pallas_call(lambda *refs: forward_kernel(n, *refs), out_shape=layer +...  267 us
    dot_general x9, matrix products, dot(): lax.dot_general(a, b, (((ca,), (cb,)), ((), ())), preferred_element_type=...  265 us
    convert_element_type x3, other arithmetic, adamw(): return ((w - 0.02 * step).astype(BF), m, v)  54.8 us
  transfers between devices with their start and end apart: 6, of which 6 were waited for; matrix products, arithmetic and copies ran while one was open for 10% of the time, Pallas kernels for 0%

profile of v1, /device:TPU:112, one launch (start us, length us, event | category | flops | bytes accessed | tf_op | source)
XLA Modules:
  0.0 1014.0 jit_solution(9118104860057666725)
XLA Ops:
  7.2 0.1 reduce-scatter.11.cloned.1.call-start
  7.3 4.2 fusion.10
  11.4 267.1 %gather_forward.1 = (bf16[1280,3456]{1,0:T(8,128)(2,1)}, bf16[1280,3456]{1,0:T(8,128)(2,1)}, bf16[3456,1280]{1,0:T(8,128)(2,1)}, bf16[1280,3456]{1,0:T(8,128)(2,...) custom-call(bf16[2048,1280]{1,0:T(8,128)(2,1)} %bitcast.42, ...), custom_call_target="tpu_custom_call" | custom-call | flops 108716359680 | bytes 300000000 | tf_op jit(solution)/shard_map/gather_forward/pallas_call | solution.py:260
  278.5 3.6 fusion.14
  282.1 0.0 copy-start
  282.1 0.6 copy-done
  282.7 39.6 %fusion.7 = (bf16[2048,3456]{1,0:T(8,128)(2,1)}, bf16[2048,3456]{1,0:T(8,128)(2,1)}) fusion(f32[2048,3456]{1,0:T(8,128)} %get-tuple-element.24, f32[2048,3456]{1,0:T(8,128)} %get-tuple-element.26, bf16[3456,1280]{1,0:T(8,128)(2,1)} %get-tuple-element.25, bf16[1,2048,1280]{2,1,0:T(8,128)(2,1)} %param.12), kind=kOutput, calls=%fused_computation.13 | convolution fusion | flops 18232639488 | bytes 99024896 | tf_op jit(solution)/shard_map/dot_general | solution.py:16
  322.3 27.2 %convolution_convert_fusion.5 = bf16[1280,3456]{1,0:T(8,128)(2,1)} fusion(bf16[2048,3456]{1,0:T(8,128)(2,1)} %get-tuple-element.27, bf16[2048,1280]{1,0:T(8,128)(2,1)} %get-tuple-element.23, f32[2048]{0:T(1024)S(1)} %fusion.38), kind=kOutput, calls=%fused_computation.25 | convolution fusion | flops 18131681280 | bytes 28254208 | tf_op jit(solution)/shard_map/dot_general | solution.py:16
  349.5 0.0 slice-start
  349.5 27.6 %convolution_convert_fusion.6 = bf16[1280,3456]{1,0:T(8,128)(2,1)} fusion(bf16[2048,3456]{1,0:T(8,128)(2,1)} %get-tuple-element.29, bf16[2048,1280]{1,0:T(8,128)(2,1)} %get-tuple-element.23, f32[2048]{0:T(1024)S(1)} %fusion.38), kind=kOutput, calls=%fused_computation.26 | convolution fusion | flops 18131681280 | bytes 28254208 | tf_op jit(solution)/shard_map/dot_general | solution.py:16
  377.1 0.0 slice-start.1
  377.1 25.5 %convolution_convert_fusion.7 = bf16[2048,1280]{1,0:T(8,128)(2,1)} fusion(bf16[2048,3456]{1,0:T(8,128)(2,1)} %get-tuple-element.29, bf16[1280,3456]{1,0:T(8,128)(2,1)} %get-tuple-element.30), kind=kOutput, calls=%fused_computation.64 | convolution fusion | flops 18122014720 | bytes 28246016 | tf_op jit(solution)/shard_map/dot_general | solution.py:16
  402.6 0.0 slice-done
  402.6 0.0 slice-done.1
  402.6 0.0 copy-start.1
  402.6 0.0 copy-start.2
  402.6 26.6 %fusion.16 = (f32[2048]{0:T(1024)S(1)}, bf16[2048,1280]{1,0:T(8,128)(2,1)}) fusion(bf16[2048,1280]{1,0:T(8,128)(2,1)S(1)} %bitcast.41, bf16[2048,1280]{1,0:T(8,128)(2,1)} %convolution_convert_fusion.7, bf16[2048,3456]{1,0:T(8,128)(2,1)} %get-tuple-element.27, bf16[1280,3456]{1,0:T(8,128)(2,1)} %get-tuple-element.28), kind=kOutput, calls=%fused_computation.48 | convolution fusion | flops 18135119872 | bytes 38739968 | tf_op jit(solution)/shard_map/dot_general | solution.py:16
  429.2 0.0 copy-done.1
  429.2 0.0 copy-done.2
  429.2 8.4 fusion.33
  437.6 25.9 %convolution_convert_fusion.4 = bf16[2048,3456]{1,0:T(8,128)(2,1)} fusion(bf16[2048,1280]{1,0:T(8,128)(2,1)} %fusion.33, bf16[3456,1280]{1,0:T(8,128)(2,1)} %get-tuple-element.31), kind=kOutput, calls=%fused_computation.24 | convolution fusion | flops 18126471168 | bytes 28246016 | tf_op jit(solution)/shard_map/dot_general | solution.py:16
  463.5 30.9 %convolution_convert_fusion.2 = bf16[1280,3456]{1,0:T(8,128)(2,1)} fusion(bf16[2048,3456]{1,0:T(8,128)(2,1)} %convolution_convert_fusion.4, f32[2048,3456]{1,0:T(8,128)} %get-tuple-element.33, f32[2048]{0:T(1024)S(1)} %add_rsqrt_fusion, bf16[1,2048,1280]{2,1,0:T(8,128)(2,1)} %param.11), kind=kOutput, calls=%fused_computation.22 | convolution fusion | flops 18181226496 | bytes 56565760 | tf_op jit(solution)/shard_map/dot_general | solution.py:16
  494.4 0.1 reduce-scatter.11.cloned.1.call-update
  494.4 0.1 reduce-scatter.13.cloned.1.call-start
  494.5 0.7 reduce-scatter.13.cloned.1.call-update
  495.3 0.1 reduce-scatter.15.cloned.1.call-start
  495.3 25.0 %convolution_convert_fusion.1 = bf16[3456,1280]{1,0:T(8,128)(2,1)} fusion(bf16[2048,3456]{1,0:T(8,128)(2,1)} %get-tuple-element.35, bf16[2048,1280]{1,0:T(8,128)(2,1)} %fusion.33), kind=kOutput, calls=%fused_computation.21 | convolution fusion | flops 18123816960 | bytes 28246016 | tf_op jit(solution)/shard_map/dot_general | solution.py:16
  520.3 0.1 reduce-scatter.15.cloned.1.call-update
  520.4 0.1 reduce-scatter.17.cloned.1.call-start
  520.4 0.6 reduce-scatter.17.cloned.1.call-update
  521.0 0.1 reduce-scatter.7.cloned.1.call-start
  521.1 36.9 %convolution_convert_fusion.3 = bf16[1280,3456]{1,0:T(8,128)(2,1)} fusion(f32[2048,3456]{1,0:T(8,128)} %get-tuple-element.33, f32[2048,3456]{1,0:T(8,128)} %get-tuple-element.32, bf16[2048,3456]{1,0:T(8,128)(2,1)} %convolution_convert_fusion.4, f32[2048]{0:T(1024)S(1)} %add_rsqrt_fusion, bf16[1,2048,1280]{2,1,0:T(8,128)(2,1)} %param.11), kind=kOutput, calls=%fused_computation.23 | convolution fusion | flops 18216615936 | bytes 84877312 | tf_op jit(solution)/shard_map/dot_general | solution.py:16
  558.0 0.1 reduce-scatter.7.cloned.1.call-update
  558.1 0.1 reduce-scatter.9.cloned.1.call-start
  558.1 0.6 reduce-scatter.9.cloned.1.call-update
  558.7 17.4 %reduce-scatter.11.cloned.1.call-done = bf16[320,3456]{1,0:T(8,128)(2,1)} async-done(((bf16[1280,3456]{1,0:T(8,128)(2,1)}), bf16[320,3456]{1,0:T(8,128)(2,1)}) %reduce-scatter.11.cloned.1.call-update) | async-done | bytes 2211856 | tf_op jit(solution)/shard_map/reduce_scatter | solution.py:291
  576.1 82.9 %reduce-scatter.13.cloned.1.call-done = bf16[320,3456]{1,0:T(8,128)(2,1)} async-done(((bf16[1280,3456]{1,0:T(8,128)(2,1)}), bf16[320,3456]{1,0:T(8,128)(2,1)}) %reduce-scatter.13.cloned.1.call-update) | async-done | bytes 2211856 | tf_op jit(solution)/shard_map/reduce_scatter | solution.py:291
  659.0 18.2 %fusion.23 = (bf16[2,320,3456]{2,1,0:T(8,128)(2,1)}, f32[2,320,3456]{2,1,0:T(8,128)}, f32[2,320,3456]{2,1,0:T(8,128)}) fusion(bf16[2,320,3456]{2,1,0:T(8,128)(2,1)} %refs_3_.1, bf16[1,320,3456]{2,1,0:T(8,128)(2,1)} %bitcast.45, bf16[1,320,3456]{2,1,0:T(8,128)(2,1)} %bitcast.44, f32[2,320,3456]{2,1,0:T(8,128)} %param.20, f32[2,320,3456]{2,1,0:T(8,128)} %param.17), kind=kLoop, calls=%fused_computation.55 | loop fusion | flops 42024960 | bytes 48660480 | tf_op jit(solution)/shard_map/convert_element_type | solution.py:33
  677.2 64.1 %reduce-scatter.15.cloned.1.call-done = bf16[864,1280]{1,0:T(8,128)(2,1)} async-done(((bf16[3456,1280]{1,0:T(8,128)(2,1)}), bf16[864,1280]{1,0:T(8,128)(2,1)}) %reduce-scatter.15.cloned.1.call-update) | async-done | bytes 2211856 | tf_op jit(solution)/shard_map/reduce_scatter | solution.py:291
  741.3 82.1 %reduce-scatter.17.cloned.1.call-done = bf16[864,1280]{1,0:T(8,128)(2,1)} async-done(((bf16[3456,1280]{1,0:T(8,128)(2,1)}), bf16[864,1280]{1,0:T(8,128)(2,1)}) %reduce-scatter.17.cloned.1.call-update) | async-done | bytes 2211856 | tf_op jit(solution)/shard_map/reduce_scatter | solution.py:291
  823.4 18.8 %fusion.27 = (bf16[2,864,1280]{2,1,0:T(8,128)(2,1)}, f32[2,864,1280]{2,1,0:T(8,128)}, f32[2,864,1280]{2,1,0:T(8,128)}) fusion(bf16[2,864,1280]{2,1,0:T(8,128)(2,1)} %refs_4_.1, bf16[1,864,1280]{2,1,0:T(8,128)(2,1)} %bitcast.47, bf16[1,864,1280]{2,1,0:T(8,128)(2,1)} %bitcast.46, f32[2,864,1280]{2,1,0:T(8,128)} %param.21, f32[2,864,1280]{2,1,0:T(8,128)} %param.18), kind=kLoop, calls=%fused_computation.59 | loop fusion | flops 42024960 | bytes 48660480 | tf_op jit(solution)/shard_map/convert_element_type | solution.py:33
  842.2 63.9 %reduce-scatter.7.cloned.1.call-done = bf16[320,3456]{1,0:T(8,128)(2,1)} async-done(((bf16[1280,3456]{1,0:T(8,128)(2,1)}), bf16[320,3456]{1,0:T(8,128)(2,1)}) %reduce-scatter.7.cloned.1.call-update) | async-done | bytes 2211856 | tf_op jit(solution)/shard_map/reduce_scatter | solution.py:291
  906.1 82.7 %reduce-scatter.9.cloned.1.call-done = bf16[320,3456]{1,0:T(8,128)(2,1)} async-done(((bf16[1280,3456]{1,0:T(8,128)(2,1)}), bf16[320,3456]{1,0:T(8,128)(2,1)}) %reduce-scatter.9.cloned.1.call-update) | async-done | bytes 2211856 | tf_op jit(solution)/shard_map/reduce_scatter | solution.py:291
  988.8 17.8 %fusion.19 = (bf16[2,320,3456]{2,1,0:T(8,128)(2,1)}, f32[2,320,3456]{2,1,0:T(8,128)}, f32[2,320,3456]{2,1,0:T(8,128)}) fusion(bf16[2,320,3456]{2,1,0:T(8,128)(2,1)} %refs_2_.1, bf16[1,320,3456]{2,1,0:T(8,128)(2,1)} %bitcast.49, bf16[1,320,3456]{2,1,0:T(8,128)(2,1)} %bitcast.48, f32[2,320,3456]{2,1,0:T(8,128)} %param.19, f32[2,320,3456]{2,1,0:T(8,128)} %param.16), kind=kLoop, calls=%fused_computation.51 | loop fusion | flops 42024960 | bytes 48660480 | tf_op jit(solution)/shard_map/convert_element_type | solution.py:33
  (4 shorter events, 0.0 us)
Async XLA Ops:
  7.2 568.9 %reduce-scatter.11.cloned.1.call-start = ((), (), s32[]{:S(2)}) async-start(), calls=%async_computation.8 | async-start | bytes 11059200 | tf_op jit(solution)/shard_map/reduce_scatter | solution.py:291
  282.1 0.6 copy-start
  349.5 53.1 %slice-start = ((s8[5242880]{0:T(1024)(128)(4,1)}), s8[1048576]{0:T(1024)(128)(4,1)S(1)}, s32[]{:S(2)}) async-start(s8[5242880]{0:T(1024)(128)(4,1)} %bitcast.40), calls=%async_computation.12 | async-start | bytes 2097152
  377.1 25.5 %slice-start.1 = ((s8[5242880]{0:T(1024)(128)(4,1)}), s8[4194304]{0:T(1024)(128)(4,1)S(1)}, s32[]{:S(2)}) async-start(s8[5242880]{0:T(1024)(128)(4,1)} %bitcast.40), calls=%async_computation.13 | async-start | bytes 8388608
  402.6 26.6 %copy-start.1 = (f32[2048]{0:T(1024)S(1)}, f32[2048]{0:T(1024)}, u32[]{:S(2)}) copy-start(f32[2048]{0:T(1024)} %copy-done) | copy-start | bytes 24580
  402.6 26.6 %copy-start.2 = (f32[2048]{0:T(1024)S(1)}, f32[2048]{0:T(1024)}, u32[]{:S(2)}) copy-start(f32[2048]{0:T(1024)} %fusion.10) | copy-start | bytes 24580
  494.4 164.5 %reduce-scatter.13.cloned.1.call-start = ((), (), s32[]{:S(2)}) async-start(), calls=%async_computation.9 | async-start | bytes 11059200 | tf_op jit(solution)/shard_map/reduce_scatter | solution.py:291
  495.3 246.0 %reduce-scatter.15.cloned.1.call-start = ((), (), s32[]{:S(2)}) async-start(), calls=%async_computation.10 | async-start | bytes 11059200 | tf_op jit(solution)/shard_map/reduce_scatter | solution.py:291
  520.4 303.0 %reduce-scatter.17.cloned.1.call-start = ((), (), s32[]{:S(2)}) async-start(), calls=%async_computation.11 | async-start | bytes 11059200 | tf_op jit(solution)/shard_map/reduce_scatter | solution.py:291
  521.0 385.1 %reduce-scatter.7.cloned.1.call-start = ((), (), s32[]{:S(2)}) async-start(), calls=%async_computation.6 | async-start | bytes 11059200 | tf_op jit(solution)/shard_map/reduce_scatter | solution.py:291
  558.1 430.7 %reduce-scatter.9.cloned.1.call-start = ((), (), s32[]{:S(2)}) async-start(), calls=%async_computation.7 | async-start | bytes 11059200 | tf_op jit(solution)/shard_map/reduce_scatter | solution.py:291
Sparse Core Ops, SparseCore 0:
  494.6 81.5 reduce-scatter.10
  579.1 79.8 reduce-scatter.12
  661.4 79.8 reduce-scatter.14
  743.5 79.8 reduce-scatter.16
  826.2 79.8 reduce-scatter.6
  908.9 79.8 reduce-scatter.8

commit v2 on v1

--- a/solution.py
+++ b/solution.py
@@ -44,8 +44,10 @@
     me = lax.axis_index("dp")
     rep = lax.axis_index("rep")
     core = lax.rem(rep, 2)
+    chip = lax.rem(rep // 2, 2)
     left, right, across = lax.rem(me + n - 1, n), lax.rem(me + 1, n), lax.rem(me + 2, n)
     to_left, to_right, to_other = {"dp": left}, {"dp": right}, {"rep": rep + 1 - 2 * core}
+    to_chip = {"rep": rep + 2 - 4 * chip}
 
     units = [(layer, kind, j) for layer in range(2) for kind, cuts in (("gu", GU_CUTS), ("d", DOWN_CUTS)) for j in range(cuts)]
 
@@ -59,53 +61,69 @@
     def at(start, size):
         return pl.ds(pl.multiple_of(start, 16), size)
 
-    def copies(unit):
+    part_at = [0]
+    for unit in range(len(units)):
+        part_at.append(part_at[-1] + len(parts(unit)))
+
+    def copies(unit, kinds):
         out = []
         for p, (w, block, cols) in enumerate(parts(unit)):
             rows = block.shape[0]
             half = rows // 2
-            a = (half // 2 + 15) // 16 * 16
-            s = core * half
-
-            def move(k, src, dst, to, p=p):
+            strip = half // 3 // 16 * 16
+            size = half - strip
+            a = (size // 2 + 15) // 16 * 16
+            s = core * half + chip * strip
+            given, got = core * half + chip * size, core * half + (1 - chip) * size
+            index = part_at[unit] + p
+
+            def move(k):
+                if k < 2:
+                    src, dst = block.at[at(s, size), cols], w.at[at(me * rows + s, size), cols]
+                    to = (to_right, to_left)[k]
+                elif k < 4:
+                    src = dst = w.at[at(left * rows + s, a), cols] if k == 2 else w.at[at(right * rows + s + a, size - a), cols]
+                    to = (to_right, to_left)[k - 2]
+                else:
+                    b = (left, right, across)[(k - 4) % 3]
+                    start, count, to = ((s, size, to_other), (given, strip, to_chip), (got, strip, to_other))[(k - 4) // 3]
+                    src = dst = w.at[at(b * rows + start, count), cols]
                 return pltpu.make_async_remote_copy(
-                    src_ref=src, dst_ref=dst, send_sem=send.at[unit, p, k], recv_sem=recv.at[unit, p, k], device_id=to, device_id_type=MESH
+                    src_ref=src, dst_ref=dst, send_sem=send.at[index, k], recv_sem=recv.at[index, k], device_id=to, device_id_type=MESH
                 )
 
-            mine, here = block.at[at(s, half), cols], w.at[at(me * rows + s, half), cols]
-            first, second = w.at[at(left * rows + s, a), cols], w.at[at(right * rows + s + a, half - a), cols]
-            trade = [w.at[at(b * rows + s, half), cols] for b in (left, right, across)]
-            out.append(
-                [move(0, mine, here, to_right), move(1, mine, here, to_left), move(2, first, first, to_right), move(3, second, second, to_left)]
-                + [move(4 + i, t, t, to_other) for i, t in enumerate(trade)]
-            )
+            out.append([move(k) for k in kinds])
         return out
 
+    def start(unit, *kinds):
+        for c in copies(unit, kinds):
+            for one in c:
+                one.start()
+
+    def arrived(unit, *kinds):
+        for c in copies(unit, kinds):
+            for one in c:
+                one.wait_recv()
+
     def A(unit):
-        for c in copies(unit):
-            c[0].start()
-            c[1].start()
+        start(unit, 0, 1)
 
     def B(unit):
-        for c in copies(unit):
-            c[0].wait_recv()
-            c[2].start()
-            c[1].wait_recv()
-            c[3].start()
-        for c in copies(unit):
-            c[4].start()
-            c[5].start()
+        arrived(unit, 0, 1)
+        start(unit, 2, 3)
+        start(unit, 7, 8)
+        start(unit, 4, 5)
 
     def C(unit):
-        for c in copies(unit):
-            c[2].wait_recv()
-            c[3].wait_recv()
-            c[6].start()
+        arrived(unit, 2, 3)
+        start(unit, 9, 6)
+
+    def E(unit):
+        arrived(unit, 7, 8, 9)
+        start(unit, 10, 11, 12)
 
     def D(unit):
-        for c in copies(unit):
-            for k in (4, 5, 6):
-                c[k].wait_recv()
+        arrived(unit, 4, 5, 6, 10, 11, 12)
 
     stay = []
     for layer in range(2):
@@ -116,9 +134,9 @@
         stay.append((wd.at[layer], hbuf.at[pl.ds(layer * rows, rows)], whole[layer][2].at[at(me * rows, rows)]))
 
     barrier = pltpu.get_barrier_semaphore()
-    for to in (to_left, to_right, to_other):
+    for to in (to_left, to_right, to_other, to_chip):
         pl.semaphore_signal(barrier, inc=1, device_id=to, device_id_type=MESH)
-    pl.semaphore_wait(barrier, 3)
+    pl.semaphore_wait(barrier, 4)
 
     A(0)
     take = pltpu.make_async_copy(x_ref, xbuf, lsem.at[6])
@@ -144,14 +162,20 @@
     B(0)
     A(1)
 
-    def ready(unit):
-        C(unit)
-        D(unit)
-
-    def hook(unit):
-        B(unit + 1)
-        if unit + 2 < len(units):
-            A(unit + 2)
+    C(0)
+    E(0)
+    B(1)
+    A(2)
+    hooks = {
+        steps - 5: lambda unit: C(unit + 1),
+        steps - 2: lambda unit: E(unit + 1),
+        steps - 1: lambda unit: (B(unit + 2), A(unit + 3) if unit + 3 < len(units) else None),
+    }
+
+    def pump(j, cuts, i, base):
+        for jj in range(cuts):
+            for step, hook in hooks.items():
+                pl.when((j == jj) & (i == step))(lambda u=base + jj, hook=hook: (hook(u), None)[1])
 
     def gate_up(layer, gate, up, base):
         wgate, wup, _ = whole[layer]
@@ -159,7 +183,7 @@
         @pl.loop(0, GU_CUTS)
         def _(j):
             for jj in range(GU_CUTS):
-                pl.when(j == jj)(lambda u=base + jj: ready(u))
+                pl.when(j == jj)(lambda u=base + jj: D(u))
             cols = pl.ds(pl.multiple_of(j * fc, 128), fc)
             ga = pltpu.make_async_copy(wgate.at[:, cols], wbuf.at[0], lsem.at[0])
             ua = pltpu.make_async_copy(wup.at[:, cols], wbuf.at[1], lsem.at[1])
@@ -170,8 +194,7 @@
 
             @pl.loop(0, steps)
             def _(i):
-                for jj in range(GU_CUTS):
-                    pl.when((j == jj) & (i == steps - 2))(lambda u=base + jj: hook(u))
+                pump(j, GU_CUTS, i, base)
                 rows = pl.ds(pl.multiple_of(i * ROWS, ROWS), ROWS)
                 slot = lax.rem(i, 2)
                 put_g = pltpu.make_async_copy(gst.at[slot], gate.at[rows, cols], ssem.at[0, slot])
@@ -202,7 +225,7 @@
     @pl.loop(0, DOWN_CUTS)
     def _(j):
         for jj in range(DOWN_CUTS):
-            pl.when(j == jj)(lambda u=GU_CUTS + jj: ready(u))
+            pl.when(j == jj)(lambda u=GU_CUTS + jj: D(u))
         cols = pl.ds(pl.multiple_of(j * dc, 128), dc)
         da = pltpu.make_async_copy(d0.at[:, cols], dbuf, lsem.at[0])
         da.start()
@@ -210,8 +233,7 @@
 
         @pl.loop(0, steps)
         def _(i):
-            for jj in range(DOWN_CUTS):
-                pl.when((j == jj) & (i == steps - 2))(lambda u=GU_CUTS + jj: hook(u))
+            pump(j, DOWN_CUTS, i, GU_CUTS)
             rows = pl.ds(pl.multiple_of(i * ROWS, ROWS), ROWS)
             hbuf[rows, cols] = xbuf[rows, cols] + dot(zbuf[rows, :], dbuf[...], 1, 0).astype(BF)
 
@@ -227,8 +249,8 @@
 
     @pl.loop(0, GRAD_CUTS)
     def _(t):
-        pl.when(t == 2)(lambda: B(last))
-        pl.when(t == 5)(lambda: C(last - 1))
+        pl.when(t == 2)(lambda: C(last))
+        pl.when(t == 4)(lambda: E(last))
         cols = pl.ds(pl.multiple_of(t * gc, 128), gc)
         slot = lax.rem(t, 2)
         put = pltpu.make_async_copy(ost.at[slot], by_d1.at[pl.ds(pl.multiple_of(t * gc, 128), gc)], osem.at[slot])
@@ -239,11 +261,10 @@
     for slot in range(2):
         pltpu.make_async_copy(ost.at[slot], by_d1.at[pl.ds(slot * gc, gc)], osem.at[slot]).wait()
     D(last - 1)
-    C(last)
     D(last)
     put_h.wait()
     for unit in range(len(units)):
-        for c in copies(unit):
+        for c in copies(unit, range(13)):
             for one in c:
                 one.wait_send()
 
@@ -252,7 +273,7 @@
     tokens, d = x.shape
     layers, _, ff = wg.shape
     fc, dc, gc = ff // GU_CUTS, d // DOWN_CUTS, ff // GRAD_CUTS
-    n_units = layers * (GU_CUTS + DOWN_CUTS)
+    n_parts = layers * (2 * GU_CUTS + DOWN_CUTS)
     out = lambda *shape, dtype=BF: jax.ShapeDtypeStruct(shape, dtype)
     layer = [out(d, ff), out(d, ff), out(ff, d)]
     pre = [out(tokens, ff, dtype=F32)] * 4
@@ -272,8 +293,8 @@
             pltpu.VMEM((2, ROWS, fc), F32),
             pltpu.VMEM((2, ROWS, fc), F32),
             pltpu.VMEM((2, gc, d), BF),
-            pltpu.SemaphoreType.DMA((n_units, 2, 7)),
-            pltpu.SemaphoreType.DMA((n_units, 2, 7)),
+            pltpu.SemaphoreType.DMA((n_parts, 13)),
+            pltpu.SemaphoreType.DMA((n_parts, 13)),
             pltpu.SemaphoreType.DMA((7,)),
             pltpu.SemaphoreType.DMA((2, 2)),
             pltpu.SemaphoreType.DMA((2,)),
@@ -282,6 +303,28 @@
         cost_estimate=pl.CostEstimate(flops=flops, bytes_accessed=300_000_000, transcendentals=0),
         name="gather_forward",
     )(x, dy, wg, wu, wd)
+
+
+def updated(layer, w, m, v, g, before=()):
+    _, rows, columns = w.shape
+    size = 64 if rows % 64 == 0 else 96
+
+    def kernel(w_ref, m_ref, v_ref, g_ref, *refs):
+        for ref, new in zip(refs[-3:], adamw(w_ref[...].astype(F32), m_ref[...], v_ref[...], g_ref[...].astype(F32)), strict=True):
+            ref[...] = new
+
+    place = pl.BlockSpec((None, size, columns), lambda i: (layer, i, 0))
+    return pl.pallas_call(
+        kernel,
+        grid=(rows // size,),
+        out_shape=[jax.ShapeDtypeStruct(t.shape, t.dtype) for t in (w, m, v)],
+        in_specs=[place, place, place, pl.BlockSpec((size, columns), lambda i: (i, 0))] + [pl.BlockSpec(memory_space=pl.ANY)] * len(before),
+        out_specs=[place] * 3,
+        input_output_aliases={4 + i: i for i in range(len(before))},
+        compiler_params=pltpu.CompilerParams(dimension_semantics=("arbitrary",)),
+        cost_estimate=pl.CostEstimate(flops=8_000_000_000, bytes_accessed=22 * rows * columns, transcendentals=rows * columns),
+        name="adamw",
+    )(w, m, v, g, *before)
 
 
 def solution(mesh):
@@ -314,8 +357,9 @@
         sum_g0 = scattered(dot(a0, by_gate0, 0, 0).astype(BF))
         sum_u0 = scattered(dot(a0, by_up0, 0, 0).astype(BF))
 
-        gradients = [jnp.stack(pair).astype(F32) for pair in ((sum_g0, sum_g1), (sum_u0, sum_u1), (sum_d0, sum_d1))]
-        new = [adamw(w.astype(F32), m, v, g) for w, m, v, g in zip(weights, m, v, gradients, strict=True)]
+        new = []
+        for w, m, v, layers in zip(weights, m, v, ((sum_g0, sum_g1), (sum_u0, sum_u1), (sum_d0, sum_d1)), strict=True):
+            new.append(updated(0, w, m, v, layers[0], updated(1, w, m, v, layers[1])))
         return tuple(one[which] for which in range(3) for one in new)
 
     states, cut = P(("rep", "dp"), None, None), P(None, "dp", None)

time: 1020 us -> 767 us (0.75)
  waiting for transfers between devices: 395 us -> 167 us
  other arithmetic: 71 us -> 13.8 us
  Pallas kernels: 267 us -> 292 us
    reduce_scatter x6, waiting for transfers between devices: 393 us -> 166 us  [scattered(): return lax.psum_scatter(g, 'dp', scatter_dimension=0, tiled=True)]
    pallas_call x0 -> x6, Pallas kernels: none -> 69.6 us  [updated(): pl.pallas_call(kernel, grid=(rows // size,), out_shape=[jax.ShapeDtypeStr...]
    convert_element_type x3 -> x0, other arithmetic: 54.8 us -> none  [adamw(): return ((w - 0.02 * step).astype(BF), m, v)]
    pallas_call x1, Pallas kernels: 267 us -> 223 us  [forward(): pl.pallas_call(lambda *refs: forward_kernel(n, *refs), out_shape=layer +...]
  transfers between devices with their start and end apart: 6 -> 6, of which waited for: 6 -> 3; matrix products, arithmetic and copies ran while one was open for 10% -> 37% of each run, Pallas kernels for 0% -> 8%
where the time goes in v2:
time: 767 us; the launch traced here: 757 us
  Pallas kernels  292 us (38%)
  matrix products  266 us (35%)
  waiting for transfers between devices  167 us (22%)
  between operations  14.7 us (2%)
  other arithmetic  13.8 us (2%)
    dot_general x9, matrix products, dot(): lax.dot_general(a, b, (((ca,), (cb,)), ((), ())), preferred_element_type=...  266 us
    pallas_call x1, Pallas kernels, forward(): pl.pallas_call(lambda *refs: forward_kernel(n, *refs), out_shape=layer +...  223 us
    reduce_scatter x6, waiting for transfers between devices, scattered(): return lax.psum_scatter(g, 'dp', scatter_dimension=0, tiled=True)  166 us
    pallas_call x6, Pallas kernels, updated(): pl.pallas_call(kernel, grid=(rows // size,), out_shape=[jax.ShapeDtypeStr...  69.6 us
  transfers between devices with their start and end apart: 6, of which 3 were waited for; matrix products, arithmetic and copies ran while one was open for 37% of the time, Pallas kernels for 8%

profile of v2, /device:TPU:112, one launch (start us, length us, event | category | flops | bytes accessed | tf_op | source)
XLA Modules:
  0.0 757.2 jit_solution(10087251140463240092)
XLA Ops:
  7.2 0.1 reduce-scatter.17.cloned.1.call-start
  7.3 222.9 %gather_forward.1 = (bf16[1280,3456]{1,0:T(8,128)(2,1)}, bf16[1280,3456]{1,0:T(8,128)(2,1)}, bf16[3456,1280]{1,0:T(8,128)(2,1)}, bf16[1280,3456]{1,0:T(8,128)(2,...) custom-call(bf16[2048,1280]{1,0:T(8,128)(2,1)} %bitcast.36, ...), custom_call_target="tpu_custom_call" | custom-call | flops 108716359680 | bytes 300000000 | tf_op jit(solution)/shard_map/gather_forward/pallas_call | solution.py:281
  230.1 0.1 reduce-scatter.17.cloned.1.call-update
  230.2 0.3 reduce-scatter.13.cloned.1.call-start
  230.5 3.7 fusion.14
  234.2 0.0 copy-start.1
  234.2 0.6 copy-done.1
  234.8 41.0 %fusion.3 = (bf16[2048,3456]{1,0:T(8,128)(2,1)}, bf16[2048,3456]{1,0:T(8,128)(2,1)}) fusion(f32[2048,3456]{1,0:T(8,128)} %get-tuple-element.42, f32[2048,3456]{1,0:T(8,128)} %get-tuple-element.44, bf16[3456,1280]{1,0:T(8,128)(2,1)} %get-tuple-element.43, bf16[1,2048,1280]{2,1,0:T(8,128)(2,1)} %param.12), kind=kOutput, calls=%fused_computation.7 | convolution fusion | flops 18232639488 | bytes 99024896 | tf_op jit(solution)/shard_map/dot_general | solution.py:16
  275.8 27.3 %convolution_convert_fusion.5 = bf16[1280,3456]{1,0:T(8,128)(2,1)} fusion(bf16[2048,3456]{1,0:T(8,128)(2,1)} %get-tuple-element.45, bf16[2048,1280]{1,0:T(8,128)(2,1)} %get-tuple-element.41, f32[2048]{0:T(1024)S(1)} %fusion.23), kind=kOutput, calls=%fused_computation.25 | convolution fusion | flops 18131681280 | bytes 28254208 | tf_op jit(solution)/shard_map/dot_general | solution.py:16
  303.1 27.7 %convolution_convert_fusion.6 = bf16[1280,3456]{1,0:T(8,128)(2,1)} fusion(bf16[2048,3456]{1,0:T(8,128)(2,1)} %get-tuple-element.47, bf16[2048,1280]{1,0:T(8,128)(2,1)} %get-tuple-element.41, f32[2048]{0:T(1024)S(1)} %fusion.23), kind=kOutput, calls=%fused_computation.26 | convolution fusion | flops 18131681280 | bytes 28254208 | tf_op jit(solution)/shard_map/dot_general | solution.py:16
  330.8 0.1 reduce-scatter.13.cloned.1.call-update
  330.8 0.1 reduce-scatter.9.cloned.1.call-start
  330.9 0.0 slice-start
  330.9 0.7 reduce-scatter.9.cloned.1.call-update
  331.6 0.1 reduce-scatter.15.cloned.1.call-start
  331.7 0.0 slice-start.1
  331.7 26.5 %convolution_convert_fusion.7 = bf16[2048,1280]{1,0:T(8,128)(2,1)} fusion(bf16[2048,3456]{1,0:T(8,128)(2,1)} %get-tuple-element.47, bf16[1280,3456]{1,0:T(8,128)(2,1)} %get-tuple-element.48), kind=kOutput, calls=%fused_computation.37 | convolution fusion | flops 18122014720 | bytes 28246016 | tf_op jit(solution)/shard_map/dot_general | solution.py:16
  358.2 0.0 slice-done
  358.2 0.0 slice-done.1
  358.2 0.0 copy-start.2
  358.2 26.5 %fusion.16 = (f32[2048]{0:T(1024)S(1)}, bf16[2048,1280]{1,0:T(8,128)(2,1)}) fusion(bf16[2048,1280]{1,0:T(8,128)(2,1)S(1)} %bitcast.35, bf16[2048,1280]{1,0:T(8,128)(2,1)} %convolution_convert_fusion.7, bf16[2048,3456]{1,0:T(8,128)(2,1)} %get-tuple-element.45, bf16[1280,3456]{1,0:T(8,128)(2,1)} %get-tuple-element.46), kind=kOutput, calls=%fused_computation.36 | convolution fusion | flops 18135119872 | bytes 38739968 | tf_op jit(solution)/shard_map/dot_general | solution.py:16
  384.7 0.0 copy-done.2
  384.7 6.1 fusion.18
  390.8 0.0 copy-start
  390.8 2.3 copy-done
  393.1 23.3 %convolution_convert_fusion.1 = bf16[3456,1280]{1,0:T(8,128)(2,1)} fusion(bf16[2048,3456]{1,0:T(8,128)(2,1)} %get-tuple-element.61, bf16[2048,1280]{1,0:T(8,128)(2,1)S(1)} %fusion.18), kind=kOutput, calls=%fused_computation.21 | convolution fusion | flops 18123816960 | bytes 28246016 | tf_op jit(solution)/shard_map/dot_general | solution.py:16
  416.4 0.1 reduce-scatter.15.cloned.1.call-update
  416.5 0.1 reduce-scatter.11.cloned.1.call-start
  416.6 4.0 fusion.10
  420.6 26.1 %convolution_convert_fusion.4 = bf16[2048,3456]{1,0:T(8,128)(2,1)} fusion(bf16[2048,1280]{1,0:T(8,128)(2,1)} %copy-done, bf16[3456,1280]{1,0:T(8,128)(2,1)} %get-tuple-element.49), kind=kOutput, calls=%fused_computation.24 | convolution fusion | flops 18126471168 | bytes 28246016 | tf_op jit(solution)/shard_map/dot_general | solution.py:16
  446.7 31.3 %convolution_convert_fusion.2 = bf16[1280,3456]{1,0:T(8,128)(2,1)} fusion(bf16[2048,3456]{1,0:T(8,128)(2,1)} %convolution_convert_fusion.4, f32[2048,3456]{1,0:T(8,128)} %get-tuple-element.51, f32[2048]{0:T(1024)S(1)} %add_rsqrt_fusion, bf16[1,2048,1280]{2,1,0:T(8,128)(2,1)} %param.11), kind=kOutput, calls=%fused_computation.22 | convolution fusion | flops 18181226496 | bytes 56565760 | tf_op jit(solution)/shard_map/dot_general | solution.py:16
  477.9 0.1 reduce-scatter.11.cloned.1.call-update
  478.0 0.1 reduce-scatter.7.cloned.1.call-start
  478.1 36.6 %convolution_convert_fusion.3 = bf16[1280,3456]{1,0:T(8,128)(2,1)} fusion(f32[2048,3456]{1,0:T(8,128)} %get-tuple-element.51, f32[2048,3456]{1,0:T(8,128)} %get-tuple-element.50, bf16[2048,3456]{1,0:T(8,128)(2,1)} %convolution_convert_fusion.4, f32[2048]{0:T(1024)S(1)} %add_rsqrt_fusion, bf16[1,2048,1280]{2,1,0:T(8,128)(2,1)} %param.11), kind=kOutput, calls=%fused_computation.23 | convolution fusion | flops 18216615936 | bytes 84877312 | tf_op jit(solution)/shard_map/dot_general | solution.py:16
  514.6 0.1 reduce-scatter.7.cloned.1.call-update
  514.7 0.0 reduce-scatter.17.cloned.1.call-done.g_ref
  514.7 12.7 %adamw.10 = (bf16[2,864,1280]{2,1,0:T(8,128)(2,1)}, f32[2,864,1280]{2,1,0:T(8,128)}, f32[2,864,1280]{2,1,0:T(8,128)}) custom-call(bf16[2,864,1280]{2,1,0:T(8,128)(2,1)} %w_ref.11, f32[2,864,1280]{2,1,0:T(8,128)} %m_ref.11, f32[2,864,1280]{2,1,0:T(8,128)} %v_ref.11, bf16[864,1280]{1,0:T(8,128)(2,1)} %reduce-scatter.17.cloned.1.call-done.g_ref), custom_call_target="tpu_custom_call" | custom-call | flops 8000000000 | bytes 24330240 | tf_op jit(solution)/shard_map/adamw/pallas_call | solution.py:317
  527.4 0.0 reduce-scatter.13.cloned.1.call-done.g_ref
  527.4 11.2 %adamw.8 = (bf16[2,320,3456]{2,1,0:T(8,128)(2,1)}, f32[2,320,3456]{2,1,0:T(8,128)}, f32[2,320,3456]{2,1,0:T(8,128)}) custom-call(bf16[2,320,3456]{2,1,0:T(8,128)(2,1)} %w_ref.9, f32[2,320,3456]{2,1,0:T(8,128)} %m_ref.9, f32[2,320,3456]{2,1,0:T(8,128)} %v_ref.9, bf16[320,3456]{1,0:T(8,128)(2,1)} %reduce-scatter.13.cloned.1.call-done.g_ref), custom_call_target="tpu_custom_call" | custom-call | flops 8000000000 | bytes 24330240 | tf_op jit(solution)/shard_map/adamw/pallas_call | solution.py:317
  538.6 0.0 reduce-scatter.9.cloned.1.call-done.g_ref
  538.6 11.3 %adamw.6 = (bf16[2,320,3456]{2,1,0:T(8,128)(2,1)}, f32[2,320,3456]{2,1,0:T(8,128)}, f32[2,320,3456]{2,1,0:T(8,128)}) custom-call(bf16[2,320,3456]{2,1,0:T(8,128)(2,1)} %w_ref.7, f32[2,320,3456]{2,1,0:T(8,128)} %m_ref.7, f32[2,320,3456]{2,1,0:T(8,128)} %v_ref.7, bf16[320,3456]{1,0:T(8,128)(2,1)} %reduce-scatter.9.cloned.1.call-done.g_ref), custom_call_target="tpu_custom_call" | custom-call | flops 8000000000 | bytes 24330240 | tf_op jit(solution)/shard_map/adamw/pallas_call | solution.py:317
  549.9 24.8 %reduce-scatter.15.cloned.1.call-done.g_ref = bf16[864,1280]{1,0:T(8,128)(2,1)} async-done(((bf16[3456,1280]{1,0:T(8,128)(2,1)}), bf16[864,1280]{1,0:T(8,128)(2,1)}) %reduce-scatter.15.cloned.1.call-update) | async-done | bytes 2211856 | tf_op jit(solution)/shard_map/reduce_scatter | solution.py:334
  574.7 12.5 %adamw.11 = (bf16[2,864,1280]{2,1,0:T(8,128)(2,1)}, f32[2,864,1280]{2,1,0:T(8,128)}, f32[2,864,1280]{2,1,0:T(8,128)}) custom-call(bf16[2,864,1280]{2,1,0:T(8,128)(2,1)} %w_ref.11, f32[2,864,1280]{2,1,0:T(8,128)} %m_ref.11, f32[2,864,1280]{2,1,0:T(8,128)} %v_ref.11, ...), custom_call_target="tpu_custom_call", output_to_operand_aliasing={{0}: (4, {}), {1}: (5, {}), {2}: (6, {})} | custom-call | flops 8000000000 | bytes 24330240 | tf_op jit(solution)/shard_map/adamw/pallas_call | solution.py:317
  587.2 69.6 %reduce-scatter.11.cloned.1.call-done.g_ref = bf16[320,3456]{1,0:T(8,128)(2,1)} async-done(((bf16[1280,3456]{1,0:T(8,128)(2,1)}), bf16[320,3456]{1,0:T(8,128)(2,1)}) %reduce-scatter.11.cloned.1.call-update) | async-done | bytes 2211856 | tf_op jit(solution)/shard_map/reduce_scatter | solution.py:334
  656.8 11.1 %adamw.9 = (bf16[2,320,3456]{2,1,0:T(8,128)(2,1)}, f32[2,320,3456]{2,1,0:T(8,128)}, f32[2,320,3456]{2,1,0:T(8,128)}) custom-call(bf16[2,320,3456]{2,1,0:T(8,128)(2,1)} %w_ref.9, f32[2,320,3456]{2,1,0:T(8,128)} %m_ref.9, f32[2,320,3456]{2,1,0:T(8,128)} %v_ref.9, ...), custom_call_target="tpu_custom_call", output_to_operand_aliasing={{0}: (4, {}), {1}: (5, {}), {2}: (6, {})} | custom-call | flops 8000000000 | bytes 24330240 | tf_op jit(solution)/shard_map/adamw/pallas_call | solution.py:317
  667.9 71.1 %reduce-scatter.7.cloned.1.call-done.g_ref = bf16[320,3456]{1,0:T(8,128)(2,1)} async-done(((bf16[1280,3456]{1,0:T(8,128)(2,1)}), bf16[320,3456]{1,0:T(8,128)(2,1)}) %reduce-scatter.7.cloned.1.call-update) | async-done | bytes 2211856 | tf_op jit(solution)/shard_map/reduce_scatter | solution.py:334
  739.0 10.9 %adamw.7 = (bf16[2,320,3456]{2,1,0:T(8,128)(2,1)}, f32[2,320,3456]{2,1,0:T(8,128)}, f32[2,320,3456]{2,1,0:T(8,128)}) custom-call(bf16[2,320,3456]{2,1,0:T(8,128)(2,1)} %w_ref.7, f32[2,320,3456]{2,1,0:T(8,128)} %m_ref.7, f32[2,320,3456]{2,1,0:T(8,128)} %v_ref.7, ...), custom_call_target="tpu_custom_call", output_to_operand_aliasing={{0}: (4, {}), {1}: (5, {}), {2}: (6, {})} | custom-call | flops 8000000000 | bytes 24330240 | tf_op jit(solution)/shard_map/adamw/pallas_call | solution.py:317
  (4 shorter events, 0.0 us)
Async XLA Ops:
  7.2 507.5 %reduce-scatter.17.cloned.1.call-start = ((), (), s32[]{:S(2)}) async-start(), calls=%async_computation.11 | async-start | bytes 11059200 | tf_op jit(solution)/shard_map/reduce_scatter | solution.py:334
  230.2 297.2 %reduce-scatter.13.cloned.1.call-start = ((), (), s32[]{:S(2)}) async-start(), calls=%async_computation.9 | async-start | bytes 11059200 | tf_op jit(solution)/shard_map/reduce_scatter | solution.py:334
  234.2 0.6 copy-start.1
  330.8 207.8 %reduce-scatter.9.cloned.1.call-start = ((), (), s32[]{:S(2)}) async-start(), calls=%async_computation.7 | async-start | bytes 11059200 | tf_op jit(solution)/shard_map/reduce_scatter | solution.py:334
  330.9 27.3 %slice-start = ((s8[5242880]{0:T(1024)(128)(4,1)}), s8[1048576]{0:T(1024)(128)(4,1)S(1)}, s32[]{:S(2)}) async-start(s8[5242880]{0:T(1024)(128)(4,1)} %bitcast.34), calls=%async_computation.12 | async-start | bytes 2097152
  331.6 243.0 %reduce-scatter.15.cloned.1.call-start = ((), (), s32[]{:S(2)}) async-start(), calls=%async_computation.10 | async-start | bytes 11059200 | tf_op jit(solution)/shard_map/reduce_scatter | solution.py:334
  331.7 26.5 %slice-start.1 = ((s8[5242880]{0:T(1024)(128)(4,1)}), s8[4194304]{0:T(1024)(128)(4,1)S(1)}, s32[]{:S(2)}) async-start(s8[5242880]{0:T(1024)(128)(4,1)} %bitcast.34), calls=%async_computation.13 | async-start | bytes 8388608
  358.2 26.5 %copy-start.2 = (f32[2048]{0:T(1024)S(1)}, f32[2048]{0:T(1024)}, u32[]{:S(2)}) copy-start(f32[2048]{0:T(1024)} %copy-done.1) | copy-start | bytes 24580
  390.8 2.4 copy-start
  416.5 240.3 %reduce-scatter.11.cloned.1.call-start = ((), (), s32[]{:S(2)}) async-start(), calls=%async_computation.8 | async-start | bytes 11059200 | tf_op jit(solution)/shard_map/reduce_scatter | solution.py:334
  478.0 261.0 %reduce-scatter.7.cloned.1.call-start = ((), (), s32[]{:S(2)}) async-start(), calls=%async_computation.6 | async-start | bytes 11059200 | tf_op jit(solution)/shard_map/reduce_scatter | solution.py:334
Sparse Core Ops, SparseCore 0:
  230.3 78.2 reduce-scatter.16
  330.9 78.6 reduce-scatter.12
  412.6 79.8 reduce-scatter.8
  494.7 79.8 reduce-scatter.14
  576.9 79.8 reduce-scatter.10
  659.0 79.8 reduce-scatter.6
